TPU v7x, 256 devices: a whole 4x4x8 slice. The times are simulated.
256 devices in a mesh: row: 4 (over x), col: 2 (over core), dp: 32 (over z, y).
Axes of the slice: x: 4, y: 4, z: 8, core: 2. Of those that a mesh axis runs over, the one named last changes fastest.
Arguments:
- out_grad: bfloat16 [32, 128, 4096], P('dp', 'col', 'row'), may hold values from -6 to 6
- saved_hidden: bfloat16 [32, 128, 14336], P('dp', 'row', 'col'), may hold values from -6 to 6
- down_weight: bfloat16 [14336, 4096], P(('col', 'dp'), 'row'), may hold values from -0.046875 to 0.046875
Outputs:
- hidden_grad: bfloat16 [32, 128, 14336], P('dp', 'row', 'col')
- weight_grad: bfloat16 [14336, 4096], P(('col', 'dp'), 'row')
All inputs are finite; a program needn't handle non-finite values.
Results may differ from a plain program's by a relative error of at most 0.009.
Values may be sent and summed in bfloat16 or wider, within the bound.
No kernel may reach another device: no remote copies, remote signals or barrier semaphores. Data moves between devices by JAX's collectives and lax.ppermute only.
A program may use at most 64 MiB of HBM per device.

v0:
```python
import jax
import jax.numpy as jnp
from jax import lax
from jax.sharding import Mesh
from jax.sharding import PartitionSpec as P

DP = ("dp_0", "dp_1")
COL_DP = ("col", "dp_0", "dp_1")


def sent_to_all(value, axis):
    devices = lax.axis_size(axis)
    return lax.all_to_all(
        jnp.broadcast_to(value[None], (devices, *value.shape)), axis, 0, 0, tiled=True
    )


def in_order(parts, dim):
    shape = list(parts.shape[1:])
    shape[dim] *= parts.shape[0]
    return jnp.moveaxis(parts, 0, dim).reshape(shape)


def gathered_copies(value, axis, dim):
    parts = sent_to_all(value, axis)
    return in_order(parts, dim)


def cut_along(value, dim, devices):
    shape = value.shape
    parts = value.reshape(*shape[:dim], devices, shape[dim] // devices, *shape[dim + 1 :])
    return jnp.moveaxis(parts, dim, 0)


def exchange_in_order(parts, axes, order):
    inside = parts.shape[1:]
    out = parts.reshape(*(lax.axis_size(a) for a in axes), *inside)
    for k in order:
        out = lax.all_to_all(out, axes[k], k, k, tiled=True)
    return out.reshape(-1, *inside)


def one_axis_at_a_time(value, axes, order, split_dim, concat_dim):
    parts = cut_along(value, split_dim, lax.axis_size(axes))
    return in_order(exchange_in_order(parts, axes, order), concat_dim)


def sent_and_summed(value, axis, dim):
    devices = lax.axis_size(axis)
    parts = lax.all_to_all(cut_along(value, dim, devices), axis, 0, 0, tiled=True)
    return jnp.sum(parts.astype(jnp.float32), axis=0)


def on_device(out_grad, saved_hidden, down_weight):
    grad_local = out_grad[0]
    hidden_local = saved_hidden[0]
    units = down_weight.shape[0]
    width = down_weight.shape[1]
    grad_replica = gathered_copies(grad_local, "col", 0)
    grad_all = lax.all_gather(grad_replica[:, None, :], DP, axis=1, tiled=True)
    tok_count = grad_all.shape[0]
    replica_count = grad_all.shape[1]
    local_tokens = hidden_local.shape[0]
    hidden_units = one_axis_at_a_time(hidden_local[:, None, :], DP, (0, 1), 2, 1)
    factor = jnp.float32(1.0) / jnp.sqrt(jnp.float32(tok_count * replica_count))
    flat_grad = grad_all.reshape(tok_count * replica_count, width)
    rows = flat_grad
    summed = sent_and_summed(
        lax.dot_general(
            rows, down_weight, (((1,), (1,)), ((), ())), preferred_element_type=jnp.float32
        ).astype(jnp.bfloat16),
        "row",
        0,
    )
    local_grad = summed.astype(jnp.bfloat16).reshape(local_tokens, replica_count, units)
    returned = lax.all_to_all(local_grad, DP, split_axis=1, concat_axis=2, tiled=True)
    hidden_grad = returned.reshape(1, local_tokens, -1)
    rows = grad_all
    left = gathered_copies(hidden_units, "row", 0).reshape(-1, units)
    right = rows.reshape(-1, width)
    total = lax.dot_general(
        left, right, (((0,), (0,)), ((), ())), preferred_element_type=jnp.float32
    )
    weight_grad = (total * factor).astype(jnp.bfloat16)
    return (hidden_grad, weight_grad)


def solution(mesh):
    split = Mesh(
        mesh.devices.reshape(mesh.shape["row"], mesh.shape["col"], 8, 4),
        ("row", "col", "dp_0", "dp_1"),
    )
    in_specs = (P(DP, "col", "row"), P(DP, "row", "col"), P(COL_DP, "row"))
    out_specs = (P(DP, "row", "col"), P(COL_DP, "row"))
    return jax.shard_map(
        on_device, mesh=split, in_specs=in_specs, out_specs=out_specs, check_vma=False
    )
```

profile of v0, /device:TPU:32, one launch (start us, length us, event | category | flops | bytes accessed | tf_op | source)
XLA Modules:
  0.0 220.8 jit_solution(18333720154147256579)
XLA Ops:
  7.2 0.0 copy-start
  7.2 0.0 all-gather.2.cloned.1.call-start
  7.2 1.0 broadcast_in_dim.15
  8.2 4.7 %all_to_all.34 = bf16[2,64,1024]{2,1,0:T(8,128)(2,1)} all-to-all(bf16[2,64,1024]{2,1,0:T(8,128)(2,1)S(1)} %broadcast_in_dim.15), channel_id=1, replica_groups=mesh['row'=4,'col'=2,'dp_0'=8,'dp_1'=4] {'col'}, dimensions={0} | all-to-all | bytes 524288 | tf_op jit(solution)/shard_map/all_to_all | solution.py:13
  12.9 0.0 all-gather.2.cloned.1.call-update
  12.9 1.8 reshape_broadcast_in_dim_squeeze.3
  14.7 0.3 copy.28
  15.0 0.4 copy.29
  15.4 27.7 %all_to_all.35 = bf16[8,4,32,1,224]{4,1,2,3,0:T(4,128)(2,1)S(1)} all-to-all(bf16[8,4,32,1,224]{4,1,2,3,0:T(4,128)(2,1)S(1)} %copy.29), channel_id=1, replica_groups=mesh['row'=4,'col'=2,'dp_0'=8,'dp_1'=4] {'dp_0'}, dimensions={0} | all-to-all | bytes 917504 | tf_op jit(solution)/shard_map/all_to_all | solution.py:39
  43.1 1.1 copy.30
  44.2 4.7 %all-to-all-start.4 = ((bf16[8,4,32,1,224]{4,0,2,3,1:T(8,128)(2,1)}), bf16[8,4,32,1,224]{4,0,2,3,1:T(8,128)(2,1)S(1)}, u32[]{:S(2)}, u32[]{:S(2)}) async-start(bf16[8,4,32,1,224]{4,0,2,3,1:T(8,128)(2,1)} %copy.30), calls=%async_computation.4 | async-start | bytes 1048576 | tf_op jit(solution)/shard_map/all_to_all | solution.py:39
  48.9 65.0 %all-gather.2.cloned.1.call-done = bf16[128,32,1024]{2,0,1:T(8,128)(2,1)} async-done(((bf16[128,1,1024]{2,0,1:T(8,128)(2,1)}), bf16[128,32,1024]{2,0,1:T(8,128)(2,1)}) %all-gather.2.cloned.1.call-update) | async-done | bytes 8388624 | tf_op jit(solution)/shard_map/all_gather | solution.py:60
  113.9 11.3 %copy.22 = bf16[128,32,1024]{2,1,0:T(8,128)(2,1)} copy(bf16[128,32,1024]{2,0,1:T(8,128)(2,1)} %all-gather.2.cloned.1.call-done) | data formatting | bytes 16777216 | tf_op jit(solution)/shard_map/all_gather | solution.py:60
  125.2 6.0 %convolution_convert_fusion = bf16[4096,224]{0,1:T(8,128)(2,1)S(1)} fusion(bf16[4096,1024]{1,0:T(8,128)(2,1)} %bitcast.21, bf16[224,1024]{1,0:T(8,128)(2,1)S(1)} %copy-done), kind=kOutput, calls=%fused_computation | convolution fusion | flops 1879965696 | bytes 10682368 | tf_op jit(solution)/shard_map/dot_general | solution.py:69
  131.2 1.5 copy.37
  132.7 0.0 all-to-all-done.4
  132.7 4.3 %all-to-all-start.1 = ((bf16[4,1024,224]{1,2,0:T(8,128)(2,1)}), bf16[4,1024,224]{1,2,0:T(8,128)(2,1)S(1)}, u32[]{:S(2)}, u32[]{:S(2)}) async-start(bf16[4,1024,224]{1,2,0:T(8,128)(2,1)} %bitcast.24), calls=%async_computation.1 | async-start | bytes 3670016 | tf_op jit(solution)/shard_map/all_to_all | solution.py:50
  137.0 0.1 copy.31
  137.1 0.3 copy.38
  137.4 22.5 %all-to-all-done.1 = bf16[4,1024,224]{1,2,0:T(8,128)(2,1)S(1)} async-done(((bf16[4,1024,224]{1,2,0:T(8,128)(2,1)}), bf16[4,1024,224]{1,2,0:T(8,128)(2,1)S(1)}, u32[]{:S(2)}, u32[]{:S(2)}) %all-to-all-start.1) | async-done | bytes 1835040 | tf_op jit(solution)/shard_map/all_to_all | solution.py:50
  159.9 1.8 broadcast_in_dim.17
  161.7 0.1 copy-done.1
  161.8 3.6 %all-to-all-start.5 = ((bf16[4,32,32,224]{3,2,1,0:T(8,128)(2,1)}), bf16[4,32,32,224]{3,2,1,0:T(8,128)(2,1)S(1)}, u32[]{:S(2)}, u32[]{:S(2)}) async-start(bf16[4,32,32,224]{3,2,1,0:T(8,128)(2,1)} %broadcast_in_dim.17), calls=%async_computation.5 | async-start | bytes 4194304 | tf_op jit(solution)/shard_map/all_to_all | solution.py:13
  165.4 1.9 reduce_sum.12
  167.3 0.2 copy.25
  167.5 1.1 copy.26
  168.6 21.7 %all-to-all-done.5 = bf16[4,32,32,224]{3,2,1,0:T(8,128)(2,1)S(1)} async-done(((bf16[4,32,32,224]{3,2,1,0:T(8,128)(2,1)}), bf16[4,32,32,224]{3,2,1,0:T(8,128)(2,1)S(1)}, u32[]{:S(2)}, u32[]{:S(2)}) %all-to-all-start.5) | async-done | bytes 1835040 | tf_op jit(solution)/shard_map/all_to_all | solution.py:13
  190.3 7.1 %all-to-all-start.2 = ((bf16[32,32,224]{2,0,1:T(8,128)(2,1)}), bf16[32,32,224]{2,0,1:T(8,128)(2,1)S(1)}, u32[]{:S(2)}, u32[]{:S(2)}) async-start(bf16[32,32,224]{2,0,1:T(8,128)(2,1)} %copy.26), calls=%async_computation.2 | async-start | bytes 1048576 | tf_op jit(solution)/shard_map/all_to_all | solution.py:76
  197.4 6.2 %fusion = bf16[224,1024]{1,0:T(8,128)(2,1)} fusion(bf16[4096,224]{1,0:T(8,128)(2,1)S(1)} %bitcast.23, bf16[4096,1024]{1,0:T(8,128)(2,1)} %bitcast.22), kind=kOutput, calls=%fused_computation.3 | convolution fusion | flops 1879506944 | bytes 10682368 | tf_op jit(solution)/shard_map/dot_general | solution.py:81
  203.7 8.3 %all-to-all-done.2 = bf16[32,32,224]{2,0,1:T(8,128)(2,1)S(1)} async-done(((bf16[32,32,224]{2,0,1:T(8,128)(2,1)}), bf16[32,32,224]{2,0,1:T(8,128)(2,1)S(1)}, u32[]{:S(2)}, u32[]{:S(2)}) %all-to-all-start.2) | async-done | bytes 458784 | tf_op jit(solution)/shard_map/all_to_all | solution.py:76
  212.0 0.3 copy.27
  212.3 1.6 reshape.31
  (2 shorter events, 0.0 us)
Async XLA Ops:
  7.2 118.0 %copy-start = (bf16[224,1024]{1,0:T(8,128)(2,1)S(1)}, bf16[224,1024]{1,0:T(8,128)(2,1)}, u32[]{:S(2)}) copy-start(bf16[224,1024]{1,0:T(8,128)(2,1)} %param.5) | copy-start | bytes 1376260
  7.2 106.7 %all-gather.2.cloned.1.call-start = ((), (), s32[]{:S(2)}) async-start(), calls=%async_computation.6 | async-start | bytes 8650752 | tf_op jit(solution)/shard_map/all_gather | solution.py:60
  44.2 88.5 %all-to-all-start.4 = ((bf16[8,4,32,1,224]{4,0,2,3,1:T(8,128)(2,1)}), bf16[8,4,32,1,224]{4,0,2,3,1:T(8,128)(2,1)S(1)}, u32[]{:S(2)}, u32[]{:S(2)}) async-start(bf16[8,4,32,1,224]{4,0,2,3,1:T(8,128)(2,1)} %copy.30), calls=%async_computation.4 | async-start | bytes 1048576 | tf_op jit(solution)/shard_map/all_to_all | solution.py:39
  132.7 27.2 %all-to-all-start.1 = ((bf16[4,1024,224]{1,2,0:T(8,128)(2,1)}), bf16[4,1024,224]{1,2,0:T(8,128)(2,1)S(1)}, u32[]{:S(2)}, u32[]{:S(2)}) async-start(bf16[4,1024,224]{1,2,0:T(8,128)(2,1)} %bitcast.24), calls=%async_computation.1 | async-start | bytes 3670016 | tf_op jit(solution)/shard_map/all_to_all | solution.py:50
  159.9 1.9 copy-start.1
  161.8 28.5 %all-to-all-start.5 = ((bf16[4,32,32,224]{3,2,1,0:T(8,128)(2,1)}), bf16[4,32,32,224]{3,2,1,0:T(8,128)(2,1)S(1)}, u32[]{:S(2)}, u32[]{:S(2)}) async-start(bf16[4,32,32,224]{3,2,1,0:T(8,128)(2,1)} %broadcast_in_dim.17), calls=%async_computation.5 | async-start | bytes 4194304 | tf_op jit(solution)/shard_map/all_to_all | solution.py:13
  190.3 21.7 %all-to-all-start.2 = ((bf16[32,32,224]{2,0,1:T(8,128)(2,1)}), bf16[32,32,224]{2,0,1:T(8,128)(2,1)S(1)}, u32[]{:S(2)}, u32[]{:S(2)}) async-start(bf16[32,32,224]{2,0,1:T(8,128)(2,1)} %copy.26), calls=%async_computation.2 | async-start | bytes 1048576 | tf_op jit(solution)/shard_map/all_to_all | solution.py:76
Sparse Core Ops, SparseCore 0:
  13.0 100.8 all-gather.1
where the time goes:
time: 221 us
  waiting for transfers between devices  118 us (53%)
  blocking collectives  32.4 us (15%)
  local copies, waits for them, and re-layouts  22.8 us (10%)
  starting transfers between devices  19.8 us (9%)
  between operations  14.1 us (6%)
  matrix products  12.2 us (6%)
    all_gather x1, waiting for transfers between devices, on_device(): grad_all = lax.all_gather(grad_replica[:, None, :], DP, axis=1, tiled=True)  65 us
    all_to_all x1, blocking collectives, exchange_in_order(): out = lax.all_to_all(out, axes[k], k, k, tiled=True)  27.7 us
    all_to_all x1, waiting for transfers between devices, sent_and_summed(): lax.all_to_all(cut_along(value, dim, devices), axis, 0, 0, tiled=True)  22.5 us
    all_to_all x1, waiting for transfers between devices, sent_to_all(): lax.all_to_all(jnp.broadcast_to(value[None], (devices, *value.shape)), ax...  21.7 us
    all_gather x1, local copies, waits for them, and re-layouts, on_device(): grad_all = lax.all_gather(grad_replica[:, None, :], DP, axis=1, tiled=True)  11.3 us
    all_to_all x1, waiting for transfers between devices, on_device(): lax.all_to_all(local_grad, DP, split_axis=1, concat_axis=2, tiled=True)  8.33 us
    all_to_all x1, starting transfers between devices, on_device(): lax.all_to_all(local_grad, DP, split_axis=1, concat_axis=2, tiled=True)  7.13 us
    dot_general x1, matrix products, on_device(): lax.dot_general(left, right, (((0,), (0,)), ((), ())), preferred_element_...  6.23 us
  transfers between devices with their start and end apart: 5, of which 4 were waited for; matrix products, arithmetic and copies ran while one was open for 15% of the time, Pallas kernels for 0%

commit v1 on v0

--- a/solution.py
+++ b/solution.py
@@ -3,6 +3,7 @@
 from jax import lax
 from jax.sharding import Mesh
 from jax.sharding import PartitionSpec as P
+from jax.lax import all_to_all, axis_size
 
 DP = ("dp_0", "dp_1")
 COL_DP = ("col", "dp_0", "dp_1")
@@ -57,7 +58,11 @@
     units = down_weight.shape[0]
     width = down_weight.shape[1]
     grad_replica = gathered_copies(grad_local, "col", 0)
-    grad_all = lax.all_gather(grad_replica[:, None, :], DP, axis=1, tiled=True)
+    deliver_slots_over_axis = lambda content: jnp.concatenate(
+        all_to_all(jnp.stack(axis_size(DP) * [content], axis=0), DP, split_axis=0, concat_axis=0),
+        axis=1,
+    )
+    grad_all = deliver_slots_over_axis(grad_replica[:, None, :])
     tok_count = grad_all.shape[0]
     replica_count = grad_all.shape[1]
     local_tokens = hidden_local.shape[0]

time: 221 us -> 347 us (1.57)
  waiting for transfers between devices: 118 us -> 239 us
  starting transfers between devices: 19.8 us -> 40.1 us
  between operations: 14.1 us -> 0.75 us
  blocking collectives: 32.4 us -> 25.1 us
  local copies, waits for them, and re-layouts: 22.8 us -> 27.8 us
    all_to_all x0 -> x1, waiting for transfers between devices: none -> 188 us  [on_device(): all_to_all(jnp.stack(axis_size(DP) * [content], axis=0), DP, split_axis=0...]
    all_gather x1 -> x0, waiting for transfers between devices: 65 us -> none  [on_device(): grad_all = lax.all_gather(grad_replica[:, None, :], DP, axis=1, tiled=True)]
    all_to_all x1, starting transfers between devices: 7.13 us -> 18.9 us  [on_device(): lax.all_to_all(local_grad, DP, split_axis=1, concat_axis=2, tiled=True)]
    all_gather x1 -> x0, local copies, waits for them, and re-layouts: 11.3 us -> none  [on_device(): grad_all = lax.all_gather(grad_replica[:, None, :], DP, axis=1, tiled=True)]
    all_to_all x0 -> x1, local copies, waits for them, and re-layouts: none -> 11.3 us  [on_device(): all_to_all(jnp.stack(axis_size(DP) * [content], axis=0), DP, split_axis=0...]
    all_to_all x0 -> x1, starting transfers between devices: none -> 6.14 us  [on_device(): all_to_all(jnp.stack(axis_size(DP) * [content], axis=0), DP, split_axis=0...]
    all_to_all x1 -> x0, blocking collectives: 4.65 us -> none  [sent_to_all(): lax.all_to_all(jnp.broadcast_to(value[None], (devices, *value.shape)), ax...]
    another operation x0 -> x1, local copies, waits for them, and re-layouts: none -> 4.29 us  [on_device(): jnp.stack(axis_size(DP) * [content], axis=0)]
  transfers between devices with their start and end apart: 5 -> 6, of which waited for: 4 -> 4; matrix products, arithmetic and copies ran while one was open for 15% -> 9% of each run, Pallas kernels for 0% -> 0%
where the time goes in v1:
time: 347 us; the launch traced here: 346 us
  waiting for transfers between devices  239 us (69%)
  starting transfers between devices  40.1 us (12%)
  local copies, waits for them, and re-layouts  27.8 us (8%)
  blocking collectives  25.1 us (7%)
  matrix products  12.3 us (4%)
    all_to_all x1, waiting for transfers between devices, on_device(): all_to_all(jnp.stack(axis_size(DP) * [content], axis=0), DP, split_axis=0...  188 us
    all_to_all x1, blocking collectives, exchange_in_order(): out = lax.all_to_all(out, axes[k], k, k, tiled=True)  25.1 us
    all_to_all x1, waiting for transfers between devices, sent_and_summed(): lax.all_to_all(cut_along(value, dim, devices), axis, 0, 0, tiled=True)  21.5 us
    all_to_all x2, waiting for transfers between devices, sent_to_all(): lax.all_to_all(jnp.broadcast_to(value[None], (devices, *value.shape)), ax...  20.5 us
    all_to_all x1, starting transfers between devices, on_device(): lax.all_to_all(local_grad, DP, split_axis=1, concat_axis=2, tiled=True)  18.9 us
    all_to_all x1, local copies, waits for them, and re-layouts, on_device(): all_to_all(jnp.stack(axis_size(DP) * [content], axis=0), DP, split_axis=0...  11.3 us
    all_to_all x1, waiting for transfers between devices, on_device(): lax.all_to_all(local_grad, DP, split_axis=1, concat_axis=2, tiled=True)  8.68 us
    all_to_all x2, starting transfers between devices, sent_to_all(): lax.all_to_all(jnp.broadcast_to(value[None], (devices, *value.shape)), ax...  7.23 us
  transfers between devices with their start and end apart: 6, of which 4 were waited for; matrix products, arithmetic and copies ran while one was open for 9% of the time, Pallas kernels for 0%

profile of v1, /device:TPU:32, one launch (start us, length us, event | category | flops | bytes accessed | tf_op | source)
XLA Modules:
  0.0 346.4 jit_solution(10180343884649840650)
XLA Ops:
  0.6 0.0 copy-start
  0.6 1.7 broadcast_in_dim.15
  2.3 3.4 all-to-all-start
  5.8 1.8 reshape_broadcast_in_dim_squeeze.3
  7.6 0.3 copy.27
  7.9 0.4 copy.28
  8.3 0.0 all-to-all-done
  8.3 25.1 %all_to_all.39 = bf16[8,4,32,1,224]{4,1,2,3,0:T(4,128)(2,1)S(1)} all-to-all(bf16[8,4,32,1,224]{4,1,2,3,0:T(4,128)(2,1)S(1)} %copy.28), channel_id=1, replica_groups=mesh['row'=4,'col'=2,'dp_0'=8,'dp_1'=4] {'dp_0'}, dimensions={0} | all-to-all | bytes 917504 | tf_op jit(solution)/shard_map/all_to_all | solution.py:40
  33.3 4.3 %stack.3 = bf16[32,128,1,1024]{3,1,2,0:T(8,128)(2,1)} broadcast(bf16[128,1024]{1,0:T(8,128)(2,1)S(1)} %bitcast.33), dimensions={1,3} | broadcast | bytes 8650752 | tf_op jit(solution)/shard_map/stack | solution.py:62
  37.6 6.1 %all-to-all-start.1 = ((bf16[32,128,1,1024]{3,1,2,0:T(8,128)(2,1)}), bf16[32,128,1,1024]{3,1,2,0:T(8,128)(2,1)}, u32[]{:S(2)}, u32[]{:S(2)}) async-start(bf16[32,128,1,1024]{3,1,2,0:T(8,128)(2,1)} %stack.3), calls=%async_computation.1 | async-start | bytes 16777216 | tf_op jit(solution)/shard_map/all_to_all | solution.py:62
  43.8 1.1 copy.29
  44.9 187.9 %all-to-all-done.1 = bf16[32,128,1,1024]{3,1,2,0:T(8,128)(2,1)} async-done(((bf16[32,128,1,1024]{3,1,2,0:T(8,128)(2,1)}), bf16[32,128,1,1024]{3,1,2,0:T(8,128)(2,1)}, u32[]{:S(2)}, u32[]{:S(2)}) %all-to-all-start.1) | async-done | bytes 8388640 | tf_op jit(solution)/shard_map/all_to_all | solution.py:62
  232.8 3.5 %all-to-all-start.5 = ((bf16[8,4,32,1,224]{4,0,2,3,1:T(8,128)(2,1)}), bf16[8,4,32,1,224]{4,0,2,3,1:T(8,128)(2,1)S(1)}, u32[]{:S(2)}, u32[]{:S(2)}) async-start(bf16[8,4,32,1,224]{4,0,2,3,1:T(8,128)(2,1)} %copy.29), calls=%async_computation.5 | async-start | bytes 1048576 | tf_op jit(solution)/shard_map/all_to_all | solution.py:40
  236.3 11.3 %copy.21 = bf16[32,128,1,1024]{3,0,1,2:T(8,128)(2,1)} copy(bf16[32,128,1,1024]{3,1,2,0:T(8,128)(2,1)} %all-to-all-done.1) | data formatting | bytes 16777216 | tf_op jit(solution)/shard_map/all_to_all | solution.py:62
  247.6 6.0 %convolution_convert_fusion = bf16[4096,224]{0,1:T(8,128)(2,1)S(1)} fusion(bf16[4096,1024]{1,0:T(8,128)(2,1)} %bitcast.23, bf16[224,1024]{1,0:T(8,128)(2,1)S(1)} %copy-done), kind=kOutput, calls=%fused_computation | convolution fusion | flops 1879965696 | bytes 10682368 | tf_op jit(solution)/shard_map/dot_general | solution.py:74
  253.6 1.5 copy.36
  255.1 4.3 %all-to-all-start.2 = ((bf16[4,1024,224]{1,2,0:T(8,128)(2,1)}), bf16[4,1024,224]{1,2,0:T(8,128)(2,1)S(1)}, u32[]{:S(2)}, u32[]{:S(2)}) async-start(bf16[4,1024,224]{1,2,0:T(8,128)(2,1)} %bitcast.26), calls=%async_computation.2 | async-start | bytes 3670016 | tf_op jit(solution)/shard_map/all_to_all | solution.py:51
  259.4 0.1 copy.30
  259.5 0.3 copy.37
  259.8 21.5 %all-to-all-done.2 = bf16[4,1024,224]{1,2,0:T(8,128)(2,1)S(1)} async-done(((bf16[4,1024,224]{1,2,0:T(8,128)(2,1)}), bf16[4,1024,224]{1,2,0:T(8,128)(2,1)S(1)}, u32[]{:S(2)}, u32[]{:S(2)}) %all-to-all-start.2) | async-done | bytes 1835040 | tf_op jit(solution)/shard_map/all_to_all | solution.py:51
  281.3 1.8 broadcast_in_dim.17
  283.1 0.1 copy-done.1
  283.2 3.8 %all-to-all-start.6 = ((bf16[4,32,32,224]{3,2,1,0:T(8,128)(2,1)}), bf16[4,32,32,224]{3,2,1,0:T(8,128)(2,1)S(1)}, u32[]{:S(2)}, u32[]{:S(2)}) async-start(bf16[4,32,32,224]{3,2,1,0:T(8,128)(2,1)} %broadcast_in_dim.17), calls=%async_computation.6 | async-start | bytes 4194304 | tf_op jit(solution)/shard_map/all_to_all | solution.py:14
  287.0 1.9 reduce_sum.12
  288.8 0.2 copy.24
  289.0 1.1 copy.25
  290.1 20.5 %all-to-all-done.6 = bf16[4,32,32,224]{3,2,1,0:T(8,128)(2,1)S(1)} async-done(((bf16[4,32,32,224]{3,2,1,0:T(8,128)(2,1)}), bf16[4,32,32,224]{3,2,1,0:T(8,128)(2,1)S(1)}, u32[]{:S(2)}, u32[]{:S(2)}) %all-to-all-start.6) | async-done | bytes 1835040 | tf_op jit(solution)/shard_map/all_to_all | solution.py:14
  310.6 18.9 %all-to-all-start.3 = ((bf16[32,32,224]{2,0,1:T(8,128)(2,1)}), bf16[32,32,224]{2,0,1:T(8,128)(2,1)S(1)}, u32[]{:S(2)}, u32[]{:S(2)}) async-start(bf16[32,32,224]{2,0,1:T(8,128)(2,1)} %copy.25), calls=%async_computation.3 | async-start | bytes 1048576 | tf_op jit(solution)/shard_map/all_to_all | solution.py:81
  329.5 6.2 %fusion = bf16[224,1024]{1,0:T(8,128)(2,1)} fusion(bf16[4096,224]{1,0:T(8,128)(2,1)S(1)} %bitcast.25, bf16[4096,1024]{1,0:T(8,128)(2,1)} %bitcast.24), kind=kOutput, calls=%fused_computation.3 | convolution fusion | flops 1879506944 | bytes 10682368 | tf_op jit(solution)/shard_map/dot_general | solution.py:86
  335.8 8.7 %all-to-all-done.3 = bf16[32,32,224]{2,0,1:T(8,128)(2,1)S(1)} async-done(((bf16[32,32,224]{2,0,1:T(8,128)(2,1)}), bf16[32,32,224]{2,0,1:T(8,128)(2,1)S(1)}, u32[]{:S(2)}, u32[]{:S(2)}) %all-to-all-start.3) | async-done | bytes 458784 | tf_op jit(solution)/shard_map/all_to_all | solution.py:81
  344.4 0.3 copy.26
  344.7 1.6 reshape.34
  (3 shorter events, 0.0 us)
Async XLA Ops:
  0.6 246.9 %copy-start = (bf16[224,1024]{1,0:T(8,128)(2,1)S(1)}, bf16[224,1024]{1,0:T(8,128)(2,1)}, u32[]{:S(2)}) copy-start(bf16[224,1024]{1,0:T(8,128)(2,1)} %param.5) | copy-start | bytes 1376260
  2.3 5.9 %all-to-all-start = ((bf16[2,64,1024]{2,1,0:T(8,128)(2,1)}), bf16[2,64,1024]{2,1,0:T(8,128)(2,1)S(1)}, u32[]{:S(2)}, u32[]{:S(2)}) async-start(bf16[2,64,1024]{2,1,0:T(8,128)(2,1)} %broadcast_in_dim.15), calls=%async_computation | async-start | bytes 524288 | tf_op jit(solution)/shard_map/all_to_all | solution.py:14
  37.6 195.1 %all-to-all-start.1 = ((bf16[32,128,1,1024]{3,1,2,0:T(8,128)(2,1)}), bf16[32,128,1,1024]{3,1,2,0:T(8,128)(2,1)}, u32[]{:S(2)}, u32[]{:S(2)}) async-start(bf16[32,128,1,1024]{3,1,2,0:T(8,128)(2,1)} %stack.3), calls=%async_computation.1 | async-start | bytes 16777216 | tf_op jit(solution)/shard_map/all_to_all | solution.py:62
  232.8 22.3 %all-to-all-start.5 = ((bf16[8,4,32,1,224]{4,0,2,3,1:T(8,128)(2,1)}), bf16[8,4,32,1,224]{4,0,2,3,1:T(8,128)(2,1)S(1)}, u32[]{:S(2)}, u32[]{:S(2)}) async-start(bf16[8,4,32,1,224]{4,0,2,3,1:T(8,128)(2,1)} %copy.29), calls=%async_computation.5 | async-start | bytes 1048576 | tf_op jit(solution)/shard_map/all_to_all | solution.py:40
  255.1 26.2 %all-to-all-start.2 = ((bf16[4,1024,224]{1,2,0:T(8,128)(2,1)}), bf16[4,1024,224]{1,2,0:T(8,128)(2,1)S(1)}, u32[]{:S(2)}, u32[]{:S(2)}) async-start(bf16[4,1024,224]{1,2,0:T(8,128)(2,1)} %bitcast.26), calls=%async_computation.2 | async-start | bytes 3670016 | tf_op jit(solution)/shard_map/all_to_all | solution.py:51
  281.3 1.9 copy-start.1
  283.2 27.4 %all-to-all-start.6 = ((bf16[4,32,32,224]{3,2,1,0:T(8,128)(2,1)}), bf16[4,32,32,224]{3,2,1,0:T(8,128)(2,1)S(1)}, u32[]{:S(2)}, u32[]{:S(2)}) async-start(bf16[4,32,32,224]{3,2,1,0:T(8,128)(2,1)} %broadcast_in_dim.17), calls=%async_computation.6 | async-start | bytes 4194304 | tf_op jit(solution)/shard_map/all_to_all | solution.py:14
  310.6 33.8 %all-to-all-start.3 = ((bf16[32,32,224]{2,0,1:T(8,128)(2,1)}), bf16[32,32,224]{2,0,1:T(8,128)(2,1)S(1)}, u32[]{:S(2)}, u32[]{:S(2)}) async-start(bf16[32,32,224]{2,0,1:T(8,128)(2,1)} %copy.25), calls=%async_computation.3 | async-start | bytes 1048576 | tf_op jit(solution)/shard_map/all_to_all | solution.py:81
